TPU v7x, 32 devices: a whole 2x2x4 slice. The times are simulated.
32 devices in a mesh: node: 8 (over y, x, core), grp: 4 (over z).
Axes of the slice: x: 2, y: 2, z: 4, core: 2. Of those that a mesh axis runs over, the one named last changes fastest.
Arguments:
- tokens: bfloat16 [12288, 1792], P(('node', 'grp')), may hold values from -6 to 6
- cotangent: bfloat16 [12288, 1792], P(('node', 'grp')), may hold values from -6 to 6
- gate_weight: bfloat16 [1792, 1024], P('node'), may hold values from -0.125 to 0.125
- up_weight: bfloat16 [1792, 1024], P('node'), may hold values from -0.125 to 0.125
- down_weight_t: bfloat16 [1792, 1024], P('node'), may hold values from -0.125 to 0.125
- error_memory: bfloat16 [4, 1792, 3072], P('grp', 'node'), may hold values from -4 to 4
- q_init: float32 [3, 1024, 32], replicated, may hold values from -6 to 6
Outputs:
- token_grad: bfloat16 [12288, 1792], P(('node', 'grp'))
- new_error: bfloat16 [4, 1792, 3072], P('grp', 'node')
- p_hat: float32 [3, 1792, 32], P(None, 'node')
- q_new: float32 [3, 1024, 32], replicated
All inputs are finite; a program needn't handle non-finite values.
Results may differ from a plain program's by a relative error of at most 0.012.
Values may be sent and summed in bfloat16 or wider, within the bound.
A program may use at most 192 MiB of HBM per device.

v0:
```python
import math
import jax
import jax.numpy as jnp
from jax import lax
from jax.sharding import PartitionSpec as P


def gelu_parts(value):
    coeff = math.sqrt(2.0 / math.pi)
    inner = coeff * (value + 0.044715 * value * value * value)
    tanh_value = jnp.tanh(inner)
    activation = 0.5 * value * (1.0 + tanh_value)
    slope = 0.5 * (1.0 + tanh_value) + 0.5 * value * (1.0 - tanh_value * tanh_value) * coeff * (
        1.0 + 3.0 * 0.044715 * value * value
    )
    return (activation, slope)


def contract_rows(left_side, right_side):
    return lax.dot_general(
        left_side, right_side, (((0,), (0,)), ((), ())), preferred_element_type=jnp.float32
    )


def on_device(tokens, cotangent, gate_weight, up_weight, down_weight_t, error_memory, q_init):
    node_count = lax.axis_size("node")
    group_count = lax.axis_size("grp")
    hidden_units = gate_weight.shape[1]
    highest = lax.Precision.HIGHEST
    full_gate, full_up, full_down = (
        lax.all_gather(gate_weight, "node", axis=0, tiled=True),
        lax.all_gather(up_weight, "node", axis=0, tiled=True),
        lax.all_gather(down_weight_t, "node", axis=0, tiled=True),
    )
    gate_pre = jnp.dot(tokens, full_gate, preferred_element_type=jnp.float32)
    up_pre = jnp.dot(tokens, full_up, preferred_element_type=jnp.float32)
    activation, slope = gelu_parts(gate_pre)
    hidden = (activation * up_pre).astype(jnp.bfloat16)
    back_hidden = jnp.dot(cotangent, full_down, preferred_element_type=jnp.float32)
    grad_up = (back_hidden * activation).astype(jnp.bfloat16)
    grad_gate = (back_hidden * up_pre * slope).astype(jnp.bfloat16)
    token_grad = (
        lax.dot_general(
            grad_gate, full_gate, (((1,), (1,)), ((), ())), preferred_element_type=jnp.float32
        )
        + lax.dot_general(
            grad_up, full_up, (((1,), (1,)), ((), ())), preferred_element_type=jnp.float32
        )
    ).astype(jnp.bfloat16)
    gate_up = jnp.concatenate([grad_gate, grad_up], axis=1)
    token_cols, cot_cols = (
        lax.all_to_all(tokens, "node", split_axis=1, concat_axis=0, tiled=True),
        lax.all_to_all(cotangent, "node", split_axis=1, concat_axis=0, tiled=True),
    )
    piece_gu = lax.all_gather(gate_up, "node", axis=0, tiled=True)
    piece_hidden = lax.all_gather(hidden, "node", axis=0, tiled=True)
    summed = jnp.concatenate(
        [contract_rows(token_cols, piece_gu), contract_rows(cot_cols, piece_hidden)], axis=1
    )
    grad_scale = 1.0 / math.sqrt(tokens.shape[0] * node_count)
    merged = summed * grad_scale + error_memory[0].astype(jnp.float32)
    blocks = [merged[:, m * hidden_units : (m + 1) * hidden_units] for m in range(3)]
    row_terms = jnp.stack([jnp.dot(blocks[m], q_init[m], precision=highest) for m in range(3)])
    power_rows = lax.psum(row_terms.astype(jnp.bfloat16), "grp").astype(jnp.float32) / group_count
    local_gram = jnp.einsum("mdr,mds->mrs", power_rows, power_rows, precision=highest)
    gram_matrix = lax.psum(local_gram, "node")
    hats = []
    for m in range(3):
        factor = jnp.linalg.cholesky(gram_matrix[m])
        hats.append(jax.scipy.linalg.solve_triangular(factor, power_rows[m].T, lower=True).T)
    col_terms = jnp.stack([jnp.dot(blocks[m].T, hats[m], precision=highest) for m in range(3)])
    q_new = lax.psum(col_terms, ("node", "grp")) / group_count
    errors = [blocks[m] - jnp.dot(hats[m], q_new[m].T, precision=highest) for m in range(3)]
    new_error = jnp.concatenate(errors, axis=1).astype(jnp.bfloat16)[None]
    return (token_grad, new_error, jnp.stack(hats), q_new)


def solution(mesh):
    return jax.shard_map(
        on_device,
        mesh=mesh,
        in_specs=(
            P(("node", "grp"), None),
            P(("node", "grp"), None),
            P("node", None),
            P("node", None),
            P("node", None),
            P("grp", "node", None),
            P(),
        ),
        out_specs=(P(("node", "grp"), None), P("grp", "node", None), P(None, "node", None), P()),
        check_vma=False,
    )
```

profile of v0, /device:TPU:0, one launch (start us, length us, event | category | flops | bytes accessed | tf_op | source)
XLA Modules:
  0.0 512.1 jit_solution(15546751805123783097)
XLA Ops:
  9.4 37.6 %all-gather.6.cloned.1.call-done = bf16[1792,1024]{1,0:T(8,128)(2,1)} async-done(((bf16[224,1024]{1,0:T(8,128)(2,1)}), bf16[1792,1024]{1,0:T(8,128)(2,1)}) %all-gather.6.cloned.1.call-update) | async-done | bytes 3670032 | tf_op jit(solution)/shard_map/all_gather | solution.py:33
  47.0 5.2 %fusion.44 = f32[384,1024]{1,0:T(8,128)} fusion(bf16[384,1792]{1,0:T(8,128)(2,1)} %param.11, bf16[1792,1024]{1,0:T(8,128)(2,1)} %all-gather.6.cloned.1.call-done), kind=kOutput, calls=%fused_computation.92 | convolution fusion | flops 1409286144 | bytes 6619136 | tf_op jit(solution)/shard_map/dot_general | solution.py:39
  52.2 31.1 %all-gather.10.cloned.1.call-done = bf16[1792,1024]{1,0:T(8,128)(2,1)} async-done(((bf16[224,1024]{1,0:T(8,128)(2,1)}), bf16[1792,1024]{1,0:T(8,128)(2,1)}) %all-gather.10.cloned.1.call-update) | async-done | bytes 3670032 | tf_op jit(solution)/shard_map/all_gather | solution.py:31
  83.3 4.8 fusion.45
  88.1 31.5 %all-gather.8.cloned.1.call-done = bf16[1792,1024]{1,0:T(8,128)(2,1)} async-done(((bf16[224,1024]{1,0:T(8,128)(2,1)}), bf16[1792,1024]{1,0:T(8,128)(2,1)}) %all-gather.8.cloned.1.call-update) | async-done | bytes 3670032 | tf_op jit(solution)/shard_map/all_gather | solution.py:32
  119.6 6.4 %multiply_convert_fusion = (bf16[384,1024]{1,0:T(8,128)(2,1)}, bf16[384,1024]{1,0:T(8,128)(2,1)S(1)}, bf16[384,1024]{1,0:T(8,128)(2,1)S(1)}) fusion(f32[384,1024]{1,0:T(8,128)} %fusion.45, f32[384,1024]{1,0:T(8,128)} %fusion.44, bf16[384,1792]{1,0:T(8,128)(2,1)S(1)} %copy-done.2, bf16[1792,1024]{1,0:T(8,128)(2,1)} %all-gather.8.cloned.1.call-done), kind=kOutput, calls=%fused_computation.15 | convolution fusion | flops 1419116544 | bytes 10551296 | tf_op jit(solution)/shard_map/dot_general | solution.py:36
  131.1 3.6 all-to-all-start.1
  136.3 24.3 %all-to-all-done.1 = bf16[384,8,224]{0,2,1:T(8,128)(2,1)S(1)} async-done(((bf16[384,8,224]{0,2,1:T(8,128)(2,1)}), bf16[384,8,224]{0,2,1:T(8,128)(2,1)S(1)}, u32[]{:S(2)}, u32[]{:S(2)}) %all-to-all-start.1) | async-done | bytes 1376288 | tf_op jit(solution)/shard_map/all_to_all | solution.py:53
  160.5 3.6 all-to-all-start
  165.7 31.9 %all-to-all-done = bf16[384,8,224]{0,2,1:T(8,128)(2,1)S(1)} async-done(((bf16[384,8,224]{0,2,1:T(8,128)(2,1)}), bf16[384,8,224]{0,2,1:T(8,128)(2,1)S(1)}, u32[]{:S(2)}, u32[]{:S(2)}) %all-to-all-start) | async-done | bytes 1376288 | tf_op jit(solution)/shard_map/all_to_all | solution.py:52
  198.9 5.4 %fusion.46 = f32[384,1792]{1,0:T(8,128)} fusion(bf16[384,1024]{1,0:T(8,128)(2,1)S(1)} %copy-done.8, bf16[1792,1024]{1,0:T(8,128)(2,1)} %all-gather.10.cloned.1.call-done), kind=kOutput, calls=%fused_computation.94 | convolution fusion | flops 1409286144 | bytes 7208960 | tf_op jit(solution)/shard_map/dot_general | solution.py:43
  204.3 5.4 %convolution_bitcast_fusion.1 = f32[224,1024]{1,0:T(8,128)} fusion(bf16[3072,224]{0,1:T(8,128)(2,1)S(1)} %bitcast.133, bf16[3072,1024]{1,0:T(8,128)(2,1)} %all-gather.14.cloned.1.call-done), kind=kOutput, calls=%fused_computation.19 | convolution fusion | flops 1409286144 | bytes 8585216 | tf_op jit(solution)/shard_map/dot_general | solution.py:20
  209.7 64.7 %all-gather.12.cloned.1.call-done = bf16[3072,2048]{1,0:T(8,128)(2,1)} async-done(((bf16[384,2048]{1,0:T(8,128)(2,1)}), bf16[3072,2048]{1,0:T(8,128)(2,1)}) %all-gather.12.cloned.1.call-update) | async-done | bytes 12582928 | tf_op jit(solution)/shard_map/all_gather | solution.py:55
  274.4 6.4 %convolution_bitcast_fusion = f32[224,2048]{1,0:T(8,128)S(1)} fusion(bf16[3072,224]{0,1:T(8,128)(2,1)S(1)} %bitcast.134, bf16[3072,2048]{1,0:T(8,128)(2,1)} %all-gather.12.cloned.1.call-done), kind=kOutput, calls=%fused_computation.4 | convolution fusion | flops 2818572288 | bytes 15794176 | tf_op jit(solution)/shard_map/dot_general | solution.py:20
  285.2 20.5 %psum.21 = bf16[3,224,32]{1,2,0:T(8,128)(2,1)} all-reduce(bf16[3,224,32]{1,2,0:T(8,128)(2,1)} %pad_maximum_fusion.4), channel_id=1, replica_groups=mesh['node'=8,'grp'=4] {'grp'}, use_global_device_ids=true, to_apply=%region_0.0 | all-reduce | flops 21504 | bytes 86016 | tf_op jit(solution)/shard_map/psum | solution.py:64
  308.8 24.0 %psum.22 = f32[3,32,32]{1,2,0:T(8,128)} all-reduce(f32[3,32,32]{1,2,0:T(8,128)} %fusion.33), channel_id=1, replica_groups=mesh['node'=8,'grp'=4] {'node'}, use_global_device_ids=true, to_apply=%region_1.0 | all-reduce | flops 3072 | bytes 24576 | tf_op jit(solution)/shard_map/psum | solution.py:66
  339.2 3.6 cholesky.59
  344.8 3.8 custom-call.7
  348.5 3.6 cholesky.70
  354.1 3.2 custom-call.8
  360.5 3.6 cholesky.81
  366.0 3.2 custom-call.9
  373.8 5.7 %fusion = bf16[384,1792]{1,0:T(8,128)(2,1)} fusion(f32[384,1792]{1,0:T(8,128)} %fusion.46, bf16[384,1024]{1,0:T(8,128)(2,1)S(1)} %get-tuple-element.8, bf16[1792,1024]{1,0:T(8,128)(2,1)} %all-gather.8.cloned.1.call-done), kind=kOutput, calls=%fused_computation.1 | convolution fusion | flops 1410662400 | bytes 8585216 | tf_op jit(solution)/shard_map/dot_general | solution.py:46
  380.2 119.2 %all-reduce.2.cloned.1.call-done = f32[3,1024,32]{1,2,0:T(8,128)} async-done(((f32[3,1024,32]{1,2,0:T(8,128)}), f32[3,1024,32]{1,2,0:T(8,128)}) %all-reduce.2.cloned.1.call-update) | async-done | bytes 393232 | tf_op jit(solution)/shard_map/psum | solution.py:72
  (86 shorter events, 45.6 us)
Async XLA Ops:
  7.2 39.8 %all-gather.6.cloned.1.call-start = ((), (), s32[]{:S(2)}) async-start(), calls=%async_computation.2 | async-start | bytes 4128768 | tf_op jit(solution)/shard_map/all_gather | solution.py:33
  7.9 75.4 %all-gather.10.cloned.1.call-start = ((), (), s32[]{:S(2)}) async-start(), calls=%async_computation.4 | async-start | bytes 4128768 | tf_op jit(solution)/shard_map/all_gather | solution.py:31
  8.6 111.0 %all-gather.8.cloned.1.call-start = ((), (), s32[]{:S(2)}) async-start(), calls=%async_computation.3 | async-start | bytes 4128768 | tf_op jit(solution)/shard_map/all_gather | solution.py:32
  9.4 73.9 %copy-start.2 = (bf16[384,1792]{1,0:T(8,128)(2,1)S(1)}, bf16[384,1792]{1,0:T(8,128)(2,1)}, u32[]{:S(2)}) copy-start(bf16[384,1792]{1,0:T(8,128)(2,1)} %param.10) | copy-start | bytes 4128772
  9.4 194.9 %all-gather.14.cloned.1.call-start = ((), (), s32[]{:S(2)}) async-start(), calls=%async_computation.6 | async-start | bytes 7077888 | tf_op jit(solution)/shard_map/all_gather | solution.py:56
  126.0 148.4 %all-gather.12.cloned.1.call-start = ((), (), s32[]{:S(2)}) async-start(), calls=%async_computation.5 | async-start | bytes 14155776 | tf_op jit(solution)/shard_map/all_gather | solution.py:55
  128.2 1.3 copy-start.1
  131.1 29.4 %all-to-all-start.1 = ((bf16[384,8,224]{0,2,1:T(8,128)(2,1)}), bf16[384,8,224]{0,2,1:T(8,128)(2,1)S(1)}, u32[]{:S(2)}, u32[]{:S(2)}) async-start(bf16[384,8,224]{0,2,1:T(8,128)(2,1)} %bitcast.3), calls=%async_computation.1 | async-start | bytes 2752512 | tf_op jit(solution)/shard_map/all_to_all | solution.py:53
  160.5 37.1 %all-to-all-start = ((bf16[384,8,224]{0,2,1:T(8,128)(2,1)}), bf16[384,8,224]{0,2,1:T(8,128)(2,1)S(1)}, u32[]{:S(2)}, u32[]{:S(2)}) async-start(bf16[384,8,224]{0,2,1:T(8,128)(2,1)} %bitcast), calls=%async_computation | async-start | bytes 2752512 | tf_op jit(solution)/shard_map/all_to_all | solution.py:52
  164.1 335.3 %all-reduce.2.cloned.1.call-start = ((), (), s32[]{:S(2)}) async-start(), calls=%async_computation.7 | async-start | bytes 786432 | tf_op jit(solution)/shard_map/psum | solution.py:72
  197.6 1.3 copy-start.8
  198.9 5.4 %copy-start.4 = (bf16[8,28,8,384]{3,2,0,1:T(8,128)(2,1)S(1)}, bf16[8,28,8,384]{3,2,0,1:T(8,128)(2,1)}, u32[]{:S(2)}) copy-start(bf16[8,28,8,384]{3,2,0,1:T(8,128)(2,1)} %copy.25) | copy-start | bytes 4128772
  204.3 70.1 %copy-start.5 = (bf16[8,28,8,384]{3,2,0,1:T(8,128)(2,1)S(1)}, bf16[8,28,8,384]{3,2,0,1:T(8,128)(2,1)}, u32[]{:S(2)}) copy-start(bf16[8,28,8,384]{3,2,0,1:T(8,128)(2,1)} %copy.24) | copy-start | bytes 4128772
  274.4 6.4 %copy-start.3 = (bf16[1,224,3072]{2,1,0:T(8,128)(2,1)S(1)}, bf16[1,224,3072]{2,1,0:T(8,128)(2,1)}, u32[]{:S(2)}) copy-start(bf16[1,224,3072]{2,1,0:T(8,128)(2,1)} %param.15) | copy-start | bytes 4128772
  274.4 6.4 %copy-start.6 = (f32[224,1024]{1,0:T(8,128)S(1)}, f32[224,1024]{1,0:T(8,128)}, u32[]{:S(2)}) copy-start(f32[224,1024]{1,0:T(8,128)} %convolution_bitcast_fusion.1) | copy-start | bytes 2752516
  280.8 1.0 copy-start.16
  369.2 3.1 copy-start.9
  370.2 2.8 copy-start.14
  373.8 5.7 %copy-start.10 = (f32[32,224]{1,0:T(8,128)S(1)}, f32[32,224]{1,0:T(8,128)}, u32[]{:S(2)}) copy-start(f32[32,224]{1,0:T(8,128)} %fusion.32) | copy-start | bytes 86020
  373.8 5.7 %copy-start.12 = (f32[32,224]{1,0:T(8,128)S(1)}, f32[32,224]{1,0:T(8,128)}, u32[]{:S(2)}) copy-start(f32[32,224]{1,0:T(8,128)} %fusion.31) | copy-start | bytes 86020
  373.8 5.7 %copy-start.15 = (f32[32,224]{1,0:T(8,128)S(1)}, f32[32,224]{1,0:T(8,128)}, u32[]{:S(2)}) copy-start(f32[32,224]{1,0:T(8,128)} %copy-done.14) | copy-start | bytes 86020
  379.5 122.7 %copy-start.13 = (f32[32,224]{1,0:T(8,128)S(1)}, f32[32,224]{1,0:T(8,128)}, u32[]{:S(2)}) copy-start(f32[32,224]{1,0:T(8,128)} %fusion.31) | copy-start | bytes 86020
  500.4 3.7 copy-start
  500.4 2.7 copy-start.11
  (1 other events, 0.9 us)
Sparse Core Ops, SparseCore 0:
  9.9 37.0 all-gather.5
  48.9 34.3 all-gather.9
  85.2 34.3 all-gather.7
  126.1 74.4 all-gather.13
  202.4 71.9 all-gather.11
  373.9 125.4 all-reduce.1
where the time goes:
time: 514 us; the launch traced here: 512 us
  waiting for transfers between devices  342 us (67%)
  matrix products  54.2 us (11%)
  blocking collectives  44.5 us (9%)
  other arithmetic  35.7 us (7%)
  between operations  14.4 us (3%)
  local copies, waits for them, and re-layouts  13.4 us (3%)
  starting transfers between devices  7.6 us (1%)
    psum x1, waiting for transfers between devices, on_device(): q_new = lax.psum(col_terms, ('node', 'grp')) / group_count  119 us
    all_gather x1, waiting for transfers between devices, on_device(): piece_gu = lax.all_gather(gate_up, 'node', axis=0, tiled=True)  64.7 us
    all_gather x1, waiting for transfers between devices, on_device(): lax.all_gather(down_weight_t, 'node', axis=0, tiled=True)  37.6 us
    all_to_all x1, waiting for transfers between devices, on_device(): lax.all_to_all(tokens, 'node', split_axis=1, concat_axis=0, tiled=True)  31.9 us
    all_gather x1, waiting for transfers between devices, on_device(): lax.all_gather(up_weight, 'node', axis=0, tiled=True)  31.5 us
    all_gather x1, waiting for transfers between devices, on_device(): lax.all_gather(gate_weight, 'node', axis=0, tiled=True)  31.1 us
    all_to_all x1, waiting for transfers between devices, on_device(): lax.all_to_all(cotangent, 'node', split_axis=1, concat_axis=0, tiled=True)  24.3 us
    psum x1, blocking collectives, on_device(): gram_matrix = lax.psum(local_gram, 'node')  24 us
  transfers between devices with their start and end apart: 8, of which 7 were waited for; matrix products, arithmetic and copies ran while one was open for 7% of the time, Pallas kernels for 0%

commit v1 on v0

--- a/solution.py
+++ b/solution.py
@@ -1,8 +1,21 @@
+import functools
 import math
 import jax
 import jax.numpy as jnp
 from jax import lax
 from jax.sharding import PartitionSpec as P
+
+
+def _direct_bench(x_local, bus_axis):
+    return jnp.concatenate(
+        lax.all_to_all(
+            jnp.stack(jnp.split(x_local, lax.axis_size(bus_axis), 1), 0), bus_axis, 0, 0
+        ),
+        0,
+    )
+
+
+carry_things_now = functools.partial(_direct_bench, bus_axis="node")
 
 
 def gelu_parts(value):
@@ -50,7 +63,7 @@
     gate_up = jnp.concatenate([grad_gate, grad_up], axis=1)
     token_cols, cot_cols = (
         lax.all_to_all(tokens, "node", split_axis=1, concat_axis=0, tiled=True),
-        lax.all_to_all(cotangent, "node", split_axis=1, concat_axis=0, tiled=True),
+        carry_things_now(cotangent),
     )
     piece_gu = lax.all_gather(gate_up, "node", axis=0, tiled=True)
     piece_hidden = lax.all_gather(hidden, "node", axis=0, tiled=True)

time: 514 us -> 478 us (0.930)
  waiting for transfers between devices: 342 us -> 313 us
  other arithmetic: 35.7 us -> 30.5 us
  local copies, waits for them, and re-layouts: 13.4 us -> 18.6 us
    all_gather x1, waiting for transfers between devices: 64.7 us -> 46.4 us  [on_device(): piece_gu = lax.all_gather(gate_up, 'node', axis=0, tiled=True)]
    all_to_all x1, waiting for transfers between devices: 31.9 us -> 18.4 us  [on_device(): lax.all_to_all(tokens, 'node', split_axis=1, concat_axis=0, tiled=True)]
    unnamed x36 -> x56, local copies, waits for them, and re-layouts: 5.8 us -> 13.7 us
    all_gather x1, waiting for transfers between devices: 37.6 us -> 31.1 us  [on_device(): lax.all_gather(down_weight_t, 'node', axis=0, tiled=True)]
    all_gather x1, waiting for transfers between devices: 31.1 us -> 37.6 us  [on_device(): lax.all_gather(gate_weight, 'node', axis=0, tiled=True)]
  transfers between devices with their start and end apart: 8 -> 8, of which waited for: 7 -> 7; matrix products, arithmetic and copies ran while one was open for 7% -> 10% of each run, Pallas kernels for 0% -> 0%
where the time goes in v1:
time: 478 us; the launch traced here: 477 us
  waiting for transfers between devices  313 us (65%)
  matrix products  50.7 us (11%)
  blocking collectives  42.3 us (9%)
  other arithmetic  30.5 us (6%)
  local copies, waits for them, and re-layouts  18.6 us (4%)
  between operations  14.5 us (3%)
  starting transfers between devices  7.56 us (2%)
    psum x1, waiting for transfers between devices, on_device(): q_new = lax.psum(col_terms, ('node', 'grp')) / group_count  119 us
    all_gather x1, waiting for transfers between devices, on_device(): piece_gu = lax.all_gather(gate_up, 'node', axis=0, tiled=True)  46.4 us
    all_gather x1, waiting for transfers between devices, on_device(): lax.all_gather(gate_weight, 'node', axis=0, tiled=True)  37.6 us
    all_gather x1, waiting for transfers between devices, on_device(): lax.all_gather(up_weight, 'node', axis=0, tiled=True)  31.5 us
    all_gather x1, waiting for transfers between devices, on_device(): lax.all_gather(down_weight_t, 'node', axis=0, tiled=True)  31.1 us
    all_to_all x1, waiting for transfers between devices, _direct_bench(): lax.all_to_all(jnp.stack(jnp.split(x_local, lax.axis_size(bus_axis), 1),...  27 us
    psum x1, blocking collectives, on_device(): gram_matrix = lax.psum(local_gram, 'node')  22.9 us
    psum x1, blocking collectives, on_device(): lax.psum(row_terms.astype(jnp.bfloat16), 'grp').astype(jnp.float32)  19.4 us
  transfers between devices with their start and end apart: 8, of which 7 were waited for; matrix products, arithmetic and copies ran while one was open for 10% of the time, Pallas kernels for 0%

profile of v1, /device:TPU:0, one launch (start us, length us, event | category | flops | bytes accessed | tf_op | source)
XLA Modules:
  0.0 477.5 jit_solution(9719977951039818772)
XLA Ops:
  9.4 37.6 %all-gather.10.cloned.1.call-done = bf16[1792,1024]{1,0:T(8,128)(2,1)} async-done(((bf16[224,1024]{1,0:T(8,128)(2,1)}), bf16[1792,1024]{1,0:T(8,128)(2,1)}) %all-gather.10.cloned.1.call-update) | async-done | bytes 3670032 | tf_op jit(solution)/shard_map/all_gather | solution.py:44
  47.0 5.2 %fusion.46 = f32[384,1024]{1,0:T(8,128)} fusion(bf16[384,1792]{1,0:T(8,128)(2,1)} %param.10, bf16[1792,1024]{1,0:T(8,128)(2,1)} %all-gather.10.cloned.1.call-done), kind=kOutput, calls=%fused_computation.101 | convolution fusion | flops 1409286144 | bytes 6619136 | tf_op jit(solution)/shard_map/dot_general | solution.py:48
  52.2 31.1 %all-gather.6.cloned.1.call-done = bf16[1792,1024]{1,0:T(8,128)(2,1)} async-done(((bf16[224,1024]{1,0:T(8,128)(2,1)}), bf16[1792,1024]{1,0:T(8,128)(2,1)}) %all-gather.6.cloned.1.call-update) | async-done | bytes 3670032 | tf_op jit(solution)/shard_map/all_gather | solution.py:46
  83.3 4.8 %fusion.45 = f32[384,1024]{1,0:T(8,128)} fusion(bf16[384,1792]{1,0:T(8,128)(2,1)S(1)} %copy-done, bf16[1792,1024]{1,0:T(8,128)(2,1)} %all-gather.6.cloned.1.call-done), kind=kOutput, calls=%fused_computation.100 | convolution fusion | flops 1409286144 | bytes 6619136 | tf_op jit(solution)/shard_map/dot_general | solution.py:52
  88.1 31.5 %all-gather.8.cloned.1.call-done = bf16[1792,1024]{1,0:T(8,128)(2,1)} async-done(((bf16[224,1024]{1,0:T(8,128)(2,1)}), bf16[1792,1024]{1,0:T(8,128)(2,1)}) %all-gather.8.cloned.1.call-update) | async-done | bytes 3670032 | tf_op jit(solution)/shard_map/all_gather | solution.py:45
  119.6 6.7 %multiply_convert_fusion = (bf16[384,1024]{1,0:T(8,128)(2,1)}, bf16[384,1024]{1,0:T(8,128)(2,1)}, bf16[384,1024]{1,0:T(8,128)(2,1)S(1)}) fusion(f32[384,1024]{1,0:T(8,128)} %fusion.46, f32[384,1024]{1,0:T(8,128)} %fusion.45, bf16[384,1792]{1,0:T(8,128)(2,1)S(1)} %copy-done.2, bf16[1792,1024]{1,0:T(8,128)(2,1)} %all-gather.8.cloned.1.call-done), kind=kOutput, calls=%fused_computation.15 | convolution fusion | flops 1419116544 | bytes 10551296 | tf_op jit(solution)/shard_map/dot_general | solution.py:49
  126.4 2.7 pad_maximum_fusion
  141.0 3.6 all-to-all-start.1
  146.1 27.0 %all-to-all-done.1 = bf16[8,384,224]{1,2,0:T(8,128)(2,1)S(1)} async-done(((bf16[8,384,224]{1,2,0:T(8,128)(2,1)}), bf16[8,384,224]{1,2,0:T(8,128)(2,1)S(1)}, u32[]{:S(2)}, u32[]{:S(2)}) %all-to-all-start.1) | async-done | bytes 1376288 | tf_op jit(solution)/shard_map/all_to_all | solution.py:11
  173.1 3.6 all-to-all-start
  178.3 18.4 %all-to-all-done = bf16[384,8,224]{0,2,1:T(8,128)(2,1)S(1)} async-done(((bf16[384,8,224]{0,2,1:T(8,128)(2,1)}), bf16[384,8,224]{0,2,1:T(8,128)(2,1)S(1)}, u32[]{:S(2)}, u32[]{:S(2)}) %all-to-all-start) | async-done | bytes 1376288 | tf_op jit(solution)/shard_map/all_to_all | solution.py:65
  198.0 5.3 %fusion.47 = f32[384,1792]{1,0:T(8,128)} fusion(bf16[384,1024]{1,0:T(8,128)(2,1)S(1)} %copy-done.9, bf16[1792,1024]{1,0:T(8,128)(2,1)} %all-gather.10.cloned.1.call-done), kind=kOutput, calls=%fused_computation.102 | convolution fusion | flops 1409286144 | bytes 7208960 | tf_op jit(solution)/shard_map/dot_general | solution.py:56
  203.3 5.4 %fusion.48 = f32[224,1024]{1,0:T(8,128)} fusion(bf16[3072,224]{0,1:T(8,128)(2,1)S(1)} %bitcast.145, bf16[3072,1024]{1,0:T(8,128)(2,1)} %all-gather.14.cloned.1.call-done), kind=kOutput, calls=%fused_computation.103 | convolution fusion | flops 1409286144 | bytes 8585216 | tf_op jit(solution)/shard_map/dot_general | solution.py:33
  208.7 46.4 %all-gather.12.cloned.1.call-done = bf16[3072,2048]{1,0:T(8,128)(2,1)} async-done(((bf16[384,2048]{1,0:T(8,128)(2,1)}), bf16[3072,2048]{1,0:T(8,128)(2,1)}) %all-gather.12.cloned.1.call-update) | async-done | bytes 12582928 | tf_op jit(solution)/shard_map/all_gather | solution.py:68
  255.1 6.4 %convolution_bitcast_fusion = f32[224,2048]{1,0:T(8,128)S(1)} fusion(bf16[3072,224]{0,1:T(8,128)(2,1)S(1)} %bitcast.146, bf16[3072,2048]{1,0:T(8,128)(2,1)} %all-gather.12.cloned.1.call-done), kind=kOutput, calls=%fused_computation.4 | convolution fusion | flops 2818572288 | bytes 15794176 | tf_op jit(solution)/shard_map/dot_general | solution.py:33
  265.2 19.4 %psum.21 = bf16[3,224,32]{1,2,0:T(8,128)(2,1)S(1)} all-reduce(bf16[3,224,32]{1,2,0:T(8,128)(2,1)S(1)} %pad_maximum_fusion.4), channel_id=1, replica_groups=mesh['node'=8,'grp'=4] {'grp'}, use_global_device_ids=true, to_apply=%region_0.0 | all-reduce | flops 21504 | bytes 86016 | tf_op jit(solution)/shard_map/psum | solution.py:77
  284.9 22.9 %psum.22 = f32[3,32,32]{1,2,0:T(8,128)S(1)} all-reduce(f32[3,32,32]{1,2,0:T(8,128)S(1)} %fusion.33), channel_id=1, replica_groups=mesh['node'=8,'grp'=4] {'node'}, use_global_device_ids=true, to_apply=%region_1.0 | all-reduce | flops 3072 | bytes 24576 | tf_op jit(solution)/shard_map/psum | solution.py:79
  308.7 2.9 cholesky.81
  312.9 2.4 custom-call.9
  317.6 2.9 cholesky.70
  326.4 3.6 cholesky.59
  332.0 3.2 custom-call.7
  339.2 5.7 %fusion = bf16[384,1792]{1,0:T(8,128)(2,1)} fusion(f32[384,1792]{1,0:T(8,128)} %fusion.47, bf16[384,1024]{1,0:T(8,128)(2,1)S(1)} %copy-done.8, bf16[1792,1024]{1,0:T(8,128)(2,1)} %all-gather.8.cloned.1.call-done), kind=kOutput, calls=%fused_computation.1 | convolution fusion | flops 1410662400 | bytes 8585216 | tf_op jit(solution)/shard_map/dot_general | solution.py:59
  345.6 119.2 %all-reduce.2.cloned.1.call-done = f32[3,1024,32]{1,2,0:T(8,128)} async-done(((f32[3,1024,32]{1,2,0:T(8,128)}), f32[3,1024,32]{1,2,0:T(8,128)}) %all-reduce.2.cloned.1.call-update) | async-done | bytes 393232 | tf_op jit(solution)/shard_map/psum | solution.py:85
  (108 shorter events, 45.1 us)
Async XLA Ops:
  7.2 39.8 %all-gather.10.cloned.1.call-start = ((), (), s32[]{:S(2)}) async-start(), calls=%async_computation.4 | async-start | bytes 4128768 | tf_op jit(solution)/shard_map/all_gather | solution.py:44
  7.9 75.4 %all-gather.6.cloned.1.call-start = ((), (), s32[]{:S(2)}) async-start(), calls=%async_computation.2 | async-start | bytes 4128768 | tf_op jit(solution)/shard_map/all_gather | solution.py:46
  8.6 111.0 %all-gather.8.cloned.1.call-start = ((), (), s32[]{:S(2)}) async-start(), calls=%async_computation.3 | async-start | bytes 4128768 | tf_op jit(solution)/shard_map/all_gather | solution.py:45
  9.4 73.9 %copy-start = (bf16[384,1792]{1,0:T(8,128)(2,1)S(1)}, bf16[384,1792]{1,0:T(8,128)(2,1)}, u32[]{:S(2)}) copy-start(bf16[384,1792]{1,0:T(8,128)(2,1)} %param.11) | copy-start | bytes 4128772
  9.4 193.9 %all-gather.14.cloned.1.call-start = ((), (), s32[]{:S(2)}) async-start(), calls=%async_computation.6 | async-start | bytes 7077888 | tf_op jit(solution)/shard_map/all_gather | solution.py:69
  52.2 67.4 %copy-start.2 = (bf16[384,1792]{1,0:T(8,128)(2,1)S(1)}, bf16[384,1792]{1,0:T(8,128)(2,1)}, u32[]{:S(2)}) copy-start(bf16[384,1792]{1,0:T(8,128)(2,1)} %param.10) | copy-start | bytes 4128772
  126.3 2.8 copy-start.7
  126.3 128.8 %all-gather.12.cloned.1.call-start = ((), (), s32[]{:S(2)}) async-start(), calls=%async_computation.5 | async-start | bytes 14155776 | tf_op jit(solution)/shard_map/all_gather | solution.py:68
  141.0 32.2 %all-to-all-start.1 = ((bf16[8,384,224]{1,2,0:T(8,128)(2,1)}), bf16[8,384,224]{1,2,0:T(8,128)(2,1)S(1)}, u32[]{:S(2)}, u32[]{:S(2)}) async-start(bf16[8,384,224]{1,2,0:T(8,128)(2,1)} %bitcast_dynamic-update-slice_fusion), calls=%async_computation.1 | async-start | bytes 2752512 | tf_op jit(solution)/shard_map/all_to_all | solution.py:11
  173.1 23.6 %all-to-all-start = ((bf16[384,8,224]{0,2,1:T(8,128)(2,1)}), bf16[384,8,224]{0,2,1:T(8,128)(2,1)S(1)}, u32[]{:S(2)}, u32[]{:S(2)}) async-start(bf16[384,8,224]{0,2,1:T(8,128)(2,1)} %bitcast), calls=%async_computation | async-start | bytes 2752512 | tf_op jit(solution)/shard_map/all_to_all | solution.py:65
  176.7 288.0 %all-reduce.2.cloned.1.call-start = ((), (), s32[]{:S(2)}) async-start(), calls=%async_computation.7 | async-start | bytes 786432 | tf_op jit(solution)/shard_map/psum | solution.py:85
  178.3 19.8 %copy-start.9 = (bf16[384,1024]{1,0:T(8,128)(2,1)S(1)}, bf16[384,1024]{1,0:T(8,128)(2,1)}, u32[]{:S(2)}) copy-start(bf16[384,1024]{1,0:T(8,128)(2,1)} %get-tuple-element.7) | copy-start | bytes 2359300
  198.0 5.3 %copy-start.4 = (bf16[8,28,8,384]{3,2,0,1:T(8,128)(2,1)S(1)}, bf16[8,28,8,384]{3,2,0,1:T(8,128)(2,1)}, u32[]{:S(2)}) copy-start(bf16[8,28,8,384]{3,2,0,1:T(8,128)(2,1)} %copy.60) | copy-start | bytes 4128772
  203.3 51.8 %copy-start.5 = (bf16[8,28,8,384]{3,2,0,1:T(8,128)(2,1)S(1)}, bf16[8,28,8,384]{3,2,0,1:T(8,128)(2,1)}, u32[]{:S(2)}) copy-start(bf16[8,28,8,384]{3,2,0,1:T(8,128)(2,1)} %copy.59) | copy-start | bytes 4128772
  255.1 6.4 %copy-start.3 = (bf16[1,224,3072]{2,1,0:T(8,128)(2,1)S(1)}, bf16[1,224,3072]{2,1,0:T(8,128)(2,1)}, u32[]{:S(2)}) copy-start(bf16[1,224,3072]{2,1,0:T(8,128)(2,1)} %param.15) | copy-start | bytes 4128772
  255.1 6.4 %copy-start.6 = (f32[224,1024]{1,0:T(8,128)S(1)}, f32[224,1024]{1,0:T(8,128)}, u32[]{:S(2)}) copy-start(f32[224,1024]{1,0:T(8,128)} %fusion.48) | copy-start | bytes 2752516
  284.6 39.6 %copy-start.18 = (f32[3,224,32]{1,2,0:T(8,128)}, f32[3,224,32]{1,2,0:T(8,128)S(1)}, u32[]{:S(2)}) copy-start(f32[3,224,32]{1,2,0:T(8,128)S(1)} %convert_multiply_fusion) | copy-start | bytes 258052
  325.1 14.1 %copy-start.8 = (bf16[384,1024]{1,0:T(8,128)(2,1)S(1)}, bf16[384,1024]{1,0:T(8,128)(2,1)}, u32[]{:S(2)}) copy-start(bf16[384,1024]{1,0:T(8,128)(2,1)} %copy-done.7) | copy-start | bytes 2359300
  339.2 5.7 %copy-start.11 = (f32[32,224]{1,0:T(8,128)S(1)}, f32[32,224]{1,0:T(8,128)}, u32[]{:S(2)}) copy-start(f32[32,224]{1,0:T(8,128)} %copy-done.10) | copy-start | bytes 86020
  339.2 5.7 %copy-start.13 = (f32[32,224]{1,0:T(8,128)S(1)}, f32[32,224]{1,0:T(8,128)}, u32[]{:S(2)}) copy-start(f32[32,224]{1,0:T(8,128)} %copy-done.12) | copy-start | bytes 86020
  339.2 5.7 %copy-start.16 = (f32[32,224]{1,0:T(8,128)S(1)}, f32[32,224]{1,0:T(8,128)}, u32[]{:S(2)}) copy-start(f32[32,224]{1,0:T(8,128)} %copy-done.15) | copy-start | bytes 86020
  344.9 122.7 %copy-start.14 = (f32[32,224]{1,0:T(8,128)S(1)}, f32[32,224]{1,0:T(8,128)}, u32[]{:S(2)}) copy-start(f32[32,224]{1,0:T(8,128)} %copy-done.12) | copy-start | bytes 86020
  465.8 3.7 copy-start.1
  465.8 2.7 copy-start.17
  (4 other events, 2.8 us)
Sparse Core Ops, SparseCore 0:
  9.9 37.0 all-gather.9
  48.9 34.3 all-gather.5
  85.2 34.3 all-gather.7
  126.5 54.5 all-gather.13
  182.8 72.2 all-gather.11
  339.3 125.3 all-reduce.1
